TPU v7x, 32 devices: a whole 2x2x4 slice. The times are simulated.
32 devices in a mesh: dp: 8 (over z, x), expert: 4 (over y, core).
Axes of the slice: x: 2, y: 2, z: 4, core: 2. Of those that a mesh axis runs over, the one named last changes fastest.
Arguments:
- tokens: bfloat16 [4096, 4096], P(('dp', 'expert')), may hold values from -6 to 6
- grad_out: bfloat16 [4096, 4096], P(('dp', 'expert')), may hold values from -6 to 6
- experts: int32 [4096, 2], P(('dp', 'expert')), may hold values from 0 to 7, all different within a row; in each aligned block of 128 rows (0 to 127, 128 to 255, ...) at most 64 rows name the same one
- gates: bfloat16 [4096, 2], P(('dp', 'expert')), may hold values from 0 to 1, as said below
- router_weight: bfloat16 [8, 4096], replicated, may hold values from -3 to 3
- saved_outputs: bfloat16 [16384, 4096], P(('dp', 'expert')), may hold values from -0.19921875 to 0.19921875
Outputs:
- input_grad: bfloat16 [4096, 4096], P(('dp', 'expert'))
- router_grad: float32 [8, 4096], replicated
- expert_grad: bfloat16 [16384, 4096], P(('dp', 'expert'))
Inputs may be any that keep to these rules, and one draw needn't show every extreme that they name: Within each aligned block of 128 tokens (the tokens of one device), no expert is named by more than 64 slots, and in some blocks an expert is named by exactly 64 slots. The two experts of a token differ. The two gates of a token are positive and add up to one, up to rounding to bfloat16.
All inputs are finite; a program needn't handle non-finite values.
Results may differ from a plain program's by a relative error of at most 0.0085.
Values may be sent and summed in bfloat16 or wider, within the bound.
A program may use at most 64 MiB of HBM per device.

v0:
```python
import jax
import jax.numpy as jnp
from jax import lax
from jax.sharding import PartitionSpec as P


def slot_positions(experts, count):
    slot_expert = experts.reshape(-1)
    onehot = (slot_expert[:, None] == jnp.arange(count, dtype=jnp.int32)[None, :]).astype(jnp.int32)
    before = jnp.cumsum(onehot, axis=0) - onehot
    return (slot_expert, jnp.sum(before * onehot, axis=1))


def local(tokens, grad_out, experts, gates, router_weight, saved_outputs):
    groups = lax.axis_size("expert")
    chosen_count = experts.shape[1]
    expert_count = router_weight.shape[0]
    held = expert_count // groups
    capacity = tokens.shape[0] // 2
    width = saved_outputs.shape[1]
    slot_expert, position = slot_positions(experts, expert_count)
    target = slot_expert % held * (groups * capacity) + slot_expert // held * capacity + position
    slot_gates = gates.reshape(-1)
    repeated = jnp.repeat(grad_out, chosen_count, axis=0)
    layout = (held, groups * capacity, width)
    returned = lax.all_to_all(
        saved_outputs.reshape(layout), "expert", split_axis=1, concat_axis=1, tiled=True
    )
    picked = returned.reshape(-1, width)[target]
    products = jnp.einsum("sd,sd->s", repeated, picked, preferred_element_type=jnp.float32)
    weighted = (slot_gates.astype(jnp.float32)[:, None] * repeated.astype(jnp.float32)).astype(
        jnp.bfloat16
    )
    buffer = jnp.zeros(saved_outputs.shape, jnp.bfloat16).at[target].set(weighted)
    expert_grad = lax.all_to_all(
        buffer.reshape(layout), "expert", split_axis=1, concat_axis=1, tiled=True
    ).reshape(-1, width)
    gate_grad = products.reshape(-1, chosen_count)
    gate_values = gates.astype(jnp.float32)
    blended = jnp.sum(gate_values * gate_grad, axis=1, keepdims=True)
    slot_grad = gate_values * (gate_grad - blended)
    onehot = (
        experts[:, :, None] == jnp.arange(expert_count, dtype=jnp.int32)[None, None, :]
    ).astype(jnp.float32)
    logit_grad = jnp.sum(onehot * slot_grad[:, :, None], axis=1).astype(jnp.bfloat16)
    partial_value = lax.dot_general(
        logit_grad, tokens, (((0,), (0,)), ((), ())), preferred_element_type=jnp.float32
    )
    summed = lax.psum(partial_value, ("dp", "expert"))
    scale_factor = float(lax.axis_size("dp") * groups * tokens.shape[0]) ** (-0.5)
    router_grad = summed * scale_factor
    input_grad = jnp.dot(logit_grad, router_weight, preferred_element_type=jnp.float32).astype(
        jnp.bfloat16
    )
    return (input_grad, router_grad, expert_grad)


def solution(mesh):
    return jax.shard_map(
        local,
        mesh=mesh,
        in_specs=(
            P(("dp", "expert"), None),
            P(("dp", "expert"), None),
            P(("dp", "expert"), None),
            P(("dp", "expert"), None),
            P(),
            P(("dp", "expert"), None),
        ),
        out_specs=(P(("dp", "expert"), None), P(), P(("dp", "expert"), None)),
        check_vma=False,
    )
```

profile of v0, /device:TPU:0, one launch (start us, length us, event | category | flops | bytes accessed | tf_op | source)
XLA Modules:
  0.0 228.8 jit_solution(14404547339752662202)
XLA Ops:
  7.2 8.7 %copy.40 = bf16[2,256,4096]{2,0,1:T(2,128)(2,1)} copy(bf16[2,256,4096]{2,1,0:T(8,128)(2,1)} %bitcast.20) | data formatting | bytes 8388608 | tf_op jit(solution)/shard_map/reshape | solution.py:27
  15.9 5.0 %all-to-all-start = ((bf16[2,256,4096]{2,0,1:T(2,128)(2,1)}), bf16[2,256,4096]{2,0,1:T(2,128)(2,1)}, u32[]{:S(2)}, u32[]{:S(2)}) async-start(bf16[2,256,4096]{2,0,1:T(2,128)(2,1)} %copy.40), calls=%async_computation | async-start | bytes 8388608 | tf_op jit(solution)/shard_map/all_to_all | solution.py:26
  21.0 0.1 eq.47
  21.2 0.1 eq.43
  21.3 0.1 reshape.177
  21.4 0.6 reduce-window.6
  22.0 0.2 slice_reduce_fusion
  22.3 3.5 %broadcast_in_dim.4 = bf16[128,2,4096]{2,1,0:T(2,128)(2,1)} broadcast(bf16[128,4096]{1,0:T(8,128)(2,1)S(1)} %copy-done.1), dimensions={0,2} | broadcast | bytes 3145728 | tf_op jit(solution)/shard_map/broadcast_in_dim | solution.py:24
  25.8 2.7 %reshape.179 = bf16[256,4096]{1,0:T(8,128)(2,1)S(1)} reshape(bf16[128,2,4096]{2,1,0:T(2,128)(2,1)} %broadcast_in_dim.4) | data formatting | bytes 4194304 | tf_op jit(solution)/shard_map/reshape | solution.py:24
  28.6 0.1 reshape.183
  28.9 6.1 %scatter_custom_fusion = bf16[512,4096]{1,0:T(8,128)(2,1)} fusion(s32[256]{0:T(256)S(1)} %bitcast.22, bf16[256,4096]{1,0:T(8,128)(2,1)S(1)} %reshape.179, f32[256]{0:T(256)S(1)} %reshape.183, bf16[]{:T(256)} %constant.44.clone.1), kind=kCustom, calls=%fused_computation.7 | custom fusion | flops 3145728 | bytes 6292482 | tf_op jit(solution)/shard_map/scatter | solution.py:34
  35.0 8.6 %copy.48 = bf16[2,256,4096]{2,0,1:T(2,128)(2,1)} copy(bf16[2,256,4096]{2,1,0:T(8,128)(2,1)} %bitcast.19) | data formatting | bytes 8388608 | tf_op jit(solution)/shard_map/reshape | solution.py:36
  43.6 26.2 %all-to-all-done = bf16[2,256,4096]{2,0,1:T(2,128)(2,1)} async-done(((bf16[2,256,4096]{2,0,1:T(2,128)(2,1)}), bf16[2,256,4096]{2,0,1:T(2,128)(2,1)}, u32[]{:S(2)}, u32[]{:S(2)}) %all-to-all-start) | async-done | bytes 4194336 | tf_op jit(solution)/shard_map/all_to_all | solution.py:26
  69.8 4.9 %all-to-all-start.1 = ((bf16[2,256,4096]{2,0,1:T(2,128)(2,1)}), bf16[2,256,4096]{2,0,1:T(2,128)(2,1)}, u32[]{:S(2)}, u32[]{:S(2)}) async-start(bf16[2,256,4096]{2,0,1:T(2,128)(2,1)} %copy.48), calls=%async_computation.1 | async-start | bytes 8388608 | tf_op jit(solution)/shard_map/all_to_all | solution.py:35
  74.8 7.1 %copy.41 = bf16[2,256,4096]{2,1,0:T(8,128)(2,1)} copy(bf16[2,256,4096]{2,0,1:T(2,128)(2,1)} %all-to-all-done) | data formatting | bytes 8388608 | tf_op jit(solution)/shard_map/all_to_all | solution.py:26
  81.9 8.0 %gather_fusion = bf16[256,4096]{1,0:T(8,128)(2,1)} fusion(bf16[512,4096]{1,0:T(8,128)(2,1)} %bitcast.18, s32[1024]{0:T(1024)S(1)} %pad_clamp_fusion), kind=kCustom, calls=%fused_computation | custom fusion | bytes 4195328 | tf_op jit(solution)/shard_map/gather | solution.py:29
  89.8 2.2 fusion
  92.1 0.1 reshape.180
  92.4 0.9 fusion.15
  93.3 1.4 convolution_convert_fusion
  94.8 28.4 %all-to-all-done.1 = bf16[2,256,4096]{2,0,1:T(2,128)(2,1)} async-done(((bf16[2,256,4096]{2,0,1:T(2,128)(2,1)}), bf16[2,256,4096]{2,0,1:T(2,128)(2,1)}, u32[]{:S(2)}, u32[]{:S(2)}) %all-to-all-start.1) | async-done | bytes 4194336 | tf_op jit(solution)/shard_map/all_to_all | solution.py:35
  123.2 7.1 %copy.49 = bf16[2,256,4096]{2,1,0:T(8,128)(2,1)} copy(bf16[2,256,4096]{2,0,1:T(2,128)(2,1)} %all-to-all-done.1) | data formatting | bytes 8388608 | tf_op jit(solution)/shard_map/all_to_all | solution.py:35
  130.3 90.1 %all-reduce.2.cloned.1.call-done = f32[8,4096]{1,0:T(8,128)} async-done(((f32[8,4096]{1,0:T(8,128)}), f32[8,4096]{1,0:T(8,128)}) %all-reduce.2.cloned.1.call-update) | async-done | bytes 131088 | tf_op jit(solution)/shard_map/psum | solution.py:49
  220.4 1.6 broadcast_multiply_fusion
  (24 shorter events, 0.6 us)
Async XLA Ops:
  7.2 85.2 %copy-start = (bf16[128,4096]{1,0:T(8,128)(2,1)S(1)}, bf16[128,4096]{1,0:T(8,128)(2,1)}, u32[]{:S(2)}) copy-start(bf16[128,4096]{1,0:T(8,128)(2,1)} %param.6) | copy-start | bytes 3145732
  15.9 5.0 %copy-start.4 = (s32[128,2]{0,1:T(2,128)S(1)}, s32[128,2]{0,1:T(2,128)}, u32[]{:S(2)}) copy-start(s32[128,2]{0,1:T(2,128)} %param.8) | copy-start | bytes 3076
  15.9 6.4 %copy-start.1 = (bf16[128,4096]{1,0:T(8,128)(2,1)S(1)}, bf16[128,4096]{1,0:T(8,128)(2,1)}, u32[]{:S(2)}) copy-start(bf16[128,4096]{1,0:T(8,128)(2,1)} %param.7) | copy-start | bytes 3145732
  15.9 53.9 %all-to-all-start = ((bf16[2,256,4096]{2,0,1:T(2,128)(2,1)}), bf16[2,256,4096]{2,0,1:T(2,128)(2,1)}, u32[]{:S(2)}, u32[]{:S(2)}) async-start(bf16[2,256,4096]{2,0,1:T(2,128)(2,1)} %copy.40), calls=%async_computation | async-start | bytes 8388608 | tf_op jit(solution)/shard_map/all_to_all | solution.py:26
  20.9 7.6 %copy-start.3 = (bf16[128,2]{0,1:T(2,128)(2,1)S(1)}, bf16[128,2]{0,1:T(2,128)(2,1)}, u32[]{:S(2)}) copy-start(bf16[128,2]{0,1:T(2,128)(2,1)} %param.9) | copy-start | bytes 1540
  69.8 53.4 %all-to-all-start.1 = ((bf16[2,256,4096]{2,0,1:T(2,128)(2,1)}), bf16[2,256,4096]{2,0,1:T(2,128)(2,1)}, u32[]{:S(2)}, u32[]{:S(2)}) async-start(bf16[2,256,4096]{2,0,1:T(2,128)(2,1)} %copy.48), calls=%async_computation.1 | async-start | bytes 8388608 | tf_op jit(solution)/shard_map/all_to_all | solution.py:35
  74.7 145.7 %all-reduce.2.cloned.1.call-start = ((), (), s32[]{:S(2)}) async-start(), calls=%async_computation.2 | async-start | bytes 262144 | tf_op jit(solution)/shard_map/psum | solution.py:49
  89.8 3.5 %copy-start.2 = (bf16[8,4096]{1,0:T(8,128)(2,1)S(1)}, bf16[8,4096]{1,0:T(8,128)(2,1)}, u32[]{:S(2)}) copy-start(bf16[8,4096]{1,0:T(8,128)(2,1)} %param.10) | copy-start | bytes 196612
Sparse Core Ops, SparseCore 0:
  93.4 126.8 all-reduce.1
where the time goes:
time: 229 us
  waiting for transfers between devices  145 us (63%)
  local copies, waits for them, and re-layouts  46.9 us (20%)
  between operations  14.2 us (6%)
  other arithmetic  10.7 us (5%)
  starting transfers between devices  9.97 us (4%)
  matrix products  2.36 us (1%)
    psum x1, waiting for transfers between devices, local(): summed = lax.psum(partial_value, ('dp', 'expert'))  90.1 us
    all_to_all x1, waiting for transfers between devices, local(): lax.all_to_all(buffer.reshape(layout), 'expert', split_axis=1, concat_axi...  28.4 us
    all_to_all x1, waiting for transfers between devices, local(): lax.all_to_all(saved_outputs.reshape(layout), 'expert', split_axis=1, con...  26.2 us
    reshape x1, local copies, waits for them, and re-layouts, local(): saved_outputs.reshape(layout)  8.69 us
    reshape x1, local copies, waits for them, and re-layouts, local(): buffer.reshape(layout)  8.56 us
    gather x1, local copies, waits for them, and re-layouts, local(): picked = returned.reshape(-1, width)[target]  7.96 us
    all_to_all x1, local copies, waits for them, and re-layouts, local(): lax.all_to_all(buffer.reshape(layout), 'expert', split_axis=1, concat_axi...  7.13 us
    all_to_all x1, local copies, waits for them, and re-layouts, local(): lax.all_to_all(saved_outputs.reshape(layout), 'expert', split_axis=1, con...  7.11 us
  transfers between devices with their start and end apart: 3, of which 3 were waited for; matrix products, arithmetic and copies ran while one was open for 22% of the time, Pallas kernels for 0%

commit v1 on v0

--- a/solution.py
+++ b/solution.py
@@ -46,7 +46,7 @@
     partial_value = lax.dot_general(
         logit_grad, tokens, (((0,), (0,)), ((), ())), preferred_element_type=jnp.float32
     )
-    summed = lax.psum(partial_value, ("dp", "expert"))
+    summed = lax.psum(lax.psum(partial_value, "dp"), "expert")
     scale_factor = float(lax.axis_size("dp") * groups * tokens.shape[0]) ** (-0.5)
     router_grad = summed * scale_factor
     input_grad = jnp.dot(logit_grad, router_weight, preferred_element_type=jnp.float32).astype(

time: 229 us -> 209 us (0.913)
  waiting for transfers between devices: 145 us -> 124 us
    all_to_all x1, waiting for transfers between devices: 28.4 us -> 0.01 us  [local(): lax.all_to_all(buffer.reshape(layout), 'expert', split_axis=1, concat_axi...]
    psum x1 -> x2, waiting for transfers between devices: 90.1 us -> 97.7 us  [local(): summed = lax.psum(lax.psum(partial_value, 'dp'), 'expert')]
  transfers between devices with their start and end apart: 3 -> 4, of which waited for: 3 -> 3; matrix products, arithmetic and copies ran while one was open for 22% -> 24% of each run, Pallas kernels for 0% -> 0%
where the time goes in v1:
time: 209 us; the launch traced here: 208 us
  waiting for transfers between devices  124 us (59%)
  local copies, waits for them, and re-layouts  46.8 us (22%)
  between operations  14.2 us (7%)
  other arithmetic  10.7 us (5%)
  starting transfers between devices  10 us (5%)
  matrix products  2.35 us (1%)
    psum x2, waiting for transfers between devices, local(): summed = lax.psum(lax.psum(partial_value, 'dp'), 'expert')  97.7 us
    all_to_all x1, waiting for transfers between devices, local(): lax.all_to_all(saved_outputs.reshape(layout), 'expert', split_axis=1, con...  26.2 us
    reshape x1, local copies, waits for them, and re-layouts, local(): saved_outputs.reshape(layout)  8.69 us
    reshape x1, local copies, waits for them, and re-layouts, local(): buffer.reshape(layout)  8.51 us
    gather x1, local copies, waits for them, and re-layouts, local(): picked = returned.reshape(-1, width)[target]  7.94 us
    all_to_all x1, local copies, waits for them, and re-layouts, local(): lax.all_to_all(saved_outputs.reshape(layout), 'expert', split_axis=1, con...  7.11 us
    all_to_all x1, local copies, waits for them, and re-layouts, local(): lax.all_to_all(buffer.reshape(layout), 'expert', split_axis=1, concat_axi...  7.11 us
    scatter x1, other arithmetic, local(): jnp.zeros(saved_outputs.shape, jnp.bfloat16).at[target].set(weighted)  6.11 us
  transfers between devices with their start and end apart: 4, of which 3 were waited for; matrix products, arithmetic and copies ran while one was open for 24% of the time, Pallas kernels for 0%

profile of v1, /device:TPU:0, one launch (start us, length us, event | category | flops | bytes accessed | tf_op | source)
XLA Modules:
  0.0 208.0 jit_solution(4459635681255743590)
XLA Ops:
  7.2 8.7 %copy.40 = bf16[2,256,4096]{2,0,1:T(2,128)(2,1)} copy(bf16[2,256,4096]{2,1,0:T(8,128)(2,1)} %bitcast.20) | data formatting | bytes 8388608 | tf_op jit(solution)/shard_map/reshape | solution.py:27
  15.9 5.0 %all-to-all-start = ((bf16[2,256,4096]{2,0,1:T(2,128)(2,1)}), bf16[2,256,4096]{2,0,1:T(2,128)(2,1)}, u32[]{:S(2)}, u32[]{:S(2)}) async-start(bf16[2,256,4096]{2,0,1:T(2,128)(2,1)} %copy.40), calls=%async_computation | async-start | bytes 8388608 | tf_op jit(solution)/shard_map/all_to_all | solution.py:26
  21.0 0.1 eq.47
  21.1 0.1 eq.43
  21.3 0.1 reshape.177
  21.4 0.6 reduce-window.6
  22.0 0.2 slice_reduce_fusion
  22.3 3.5 %broadcast_in_dim.4 = bf16[128,2,4096]{2,1,0:T(2,128)(2,1)} broadcast(bf16[128,4096]{1,0:T(8,128)(2,1)S(1)} %copy-done.1), dimensions={0,2} | broadcast | bytes 3145728 | tf_op jit(solution)/shard_map/broadcast_in_dim | solution.py:24
  25.8 2.7 %reshape.179 = bf16[256,4096]{1,0:T(8,128)(2,1)S(1)} reshape(bf16[128,2,4096]{2,1,0:T(2,128)(2,1)} %broadcast_in_dim.4) | data formatting | bytes 4194304 | tf_op jit(solution)/shard_map/reshape | solution.py:24
  28.6 0.1 reshape.183
  28.9 6.1 %scatter_custom_fusion = bf16[512,4096]{1,0:T(8,128)(2,1)} fusion(s32[256]{0:T(256)S(1)} %bitcast.22, bf16[256,4096]{1,0:T(8,128)(2,1)S(1)} %reshape.179, f32[256]{0:T(256)S(1)} %reshape.183, bf16[]{:T(256)} %constant.44.clone.1), kind=kCustom, calls=%fused_computation.7 | custom fusion | flops 3145728 | bytes 6292482 | tf_op jit(solution)/shard_map/scatter | solution.py:34
  35.0 8.5 %copy.48 = bf16[2,256,4096]{2,0,1:T(2,128)(2,1)} copy(bf16[2,256,4096]{2,1,0:T(8,128)(2,1)} %bitcast.19) | data formatting | bytes 8388608 | tf_op jit(solution)/shard_map/reshape | solution.py:36
  43.5 26.2 %all-to-all-done = bf16[2,256,4096]{2,0,1:T(2,128)(2,1)} async-done(((bf16[2,256,4096]{2,0,1:T(2,128)(2,1)}), bf16[2,256,4096]{2,0,1:T(2,128)(2,1)}, u32[]{:S(2)}, u32[]{:S(2)}) %all-to-all-start) | async-done | bytes 4194336 | tf_op jit(solution)/shard_map/all_to_all | solution.py:26
  69.8 4.9 %all-to-all-start.1 = ((bf16[2,256,4096]{2,0,1:T(2,128)(2,1)}), bf16[2,256,4096]{2,0,1:T(2,128)(2,1)}, u32[]{:S(2)}, u32[]{:S(2)}) async-start(bf16[2,256,4096]{2,0,1:T(2,128)(2,1)} %copy.48), calls=%async_computation.1 | async-start | bytes 8388608 | tf_op jit(solution)/shard_map/all_to_all | solution.py:35
  74.8 7.1 %copy.41 = bf16[2,256,4096]{2,1,0:T(8,128)(2,1)} copy(bf16[2,256,4096]{2,0,1:T(2,128)(2,1)} %all-to-all-done) | data formatting | bytes 8388608 | tf_op jit(solution)/shard_map/all_to_all | solution.py:26
  81.9 7.9 %gather_fusion = bf16[256,4096]{1,0:T(8,128)(2,1)} fusion(bf16[512,4096]{1,0:T(8,128)(2,1)} %bitcast.18, s32[1024]{0:T(1024)S(1)} %pad_clamp_fusion), kind=kCustom, calls=%fused_computation | custom fusion | bytes 4195328 | tf_op jit(solution)/shard_map/gather | solution.py:29
  89.8 2.2 %fusion = f32[256]{0:T(256)S(1)} fusion(bf16[256,4096]{1,0:T(8,128)(2,1)S(1)} %reshape.179, bf16[256,4096]{1,0:T(8,128)(2,1)} %gather_fusion), kind=kLoop, calls=%fused_computation.5 | loop fusion | flops 4194048 | bytes 4195328 | tf_op jit(solution)/shard_map/sd,sd->s/dot_general | solution.py:30
  92.1 0.1 reshape.180
  92.3 0.9 fusion.15
  93.3 73.1 %all-reduce.3.cloned.1.call-done = f32[8,4096]{1,0:T(8,128)} async-done(((f32[8,4096]{1,0:T(8,128)}), f32[8,4096]{1,0:T(8,128)}) %all-reduce.3.cloned.1.call-update) | async-done | bytes 131088 | tf_op jit(solution)/shard_map/psum | solution.py:49
  166.4 1.4 convolution_convert_fusion
  167.9 7.1 %copy.49 = bf16[2,256,4096]{2,1,0:T(8,128)(2,1)} copy(bf16[2,256,4096]{2,0,1:T(2,128)(2,1)} %all-to-all-done.1) | data formatting | bytes 8388608 | tf_op jit(solution)/shard_map/all_to_all | solution.py:35
  175.0 24.6 %all-reduce.5.cloned.1.call-done = f32[8,4096]{1,0:T(8,128)} async-done(((f32[8,4096]{1,0:T(8,128)}), f32[8,4096]{1,0:T(8,128)}) %all-reduce.5.cloned.1.call-update) | async-done | bytes 131088 | tf_op jit(solution)/shard_map/psum | solution.py:49
  199.6 1.6 broadcast_multiply_fusion
  (27 shorter events, 0.6 us)
Async XLA Ops:
  7.2 85.2 %copy-start = (bf16[128,4096]{1,0:T(8,128)(2,1)S(1)}, bf16[128,4096]{1,0:T(8,128)(2,1)}, u32[]{:S(2)}) copy-start(bf16[128,4096]{1,0:T(8,128)(2,1)} %param.6) | copy-start | bytes 3145732
  15.9 5.0 %copy-start.4 = (s32[128,2]{0,1:T(2,128)S(1)}, s32[128,2]{0,1:T(2,128)}, u32[]{:S(2)}) copy-start(s32[128,2]{0,1:T(2,128)} %param.8) | copy-start | bytes 3076
  15.9 6.4 %copy-start.1 = (bf16[128,4096]{1,0:T(8,128)(2,1)S(1)}, bf16[128,4096]{1,0:T(8,128)(2,1)}, u32[]{:S(2)}) copy-start(bf16[128,4096]{1,0:T(8,128)(2,1)} %param.7) | copy-start | bytes 3145732
  15.9 53.9 %all-to-all-start = ((bf16[2,256,4096]{2,0,1:T(2,128)(2,1)}), bf16[2,256,4096]{2,0,1:T(2,128)(2,1)}, u32[]{:S(2)}, u32[]{:S(2)}) async-start(bf16[2,256,4096]{2,0,1:T(2,128)(2,1)} %copy.40), calls=%async_computation | async-start | bytes 8388608 | tf_op jit(solution)/shard_map/all_to_all | solution.py:26
  20.9 7.6 %copy-start.3 = (bf16[128,2]{0,1:T(2,128)(2,1)S(1)}, bf16[128,2]{0,1:T(2,128)(2,1)}, u32[]{:S(2)}) copy-start(bf16[128,2]{0,1:T(2,128)(2,1)} %param.9) | copy-start | bytes 1540
  69.8 98.1 %all-to-all-start.1 = ((bf16[2,256,4096]{2,0,1:T(2,128)(2,1)}), bf16[2,256,4096]{2,0,1:T(2,128)(2,1)}, u32[]{:S(2)}, u32[]{:S(2)}) async-start(bf16[2,256,4096]{2,0,1:T(2,128)(2,1)} %copy.48), calls=%async_computation.1 | async-start | bytes 8388608 | tf_op jit(solution)/shard_map/all_to_all | solution.py:35
  74.7 91.7 %all-reduce.3.cloned.1.call-start = ((), (), s32[]{:S(2)}) async-start(), calls=%async_computation.2 | async-start | bytes 262144 | tf_op jit(solution)/shard_map/psum | solution.py:49
  89.8 76.6 %copy-start.2 = (bf16[8,4096]{1,0:T(8,128)(2,1)S(1)}, bf16[8,4096]{1,0:T(8,128)(2,1)}, u32[]{:S(2)}) copy-start(bf16[8,4096]{1,0:T(8,128)(2,1)} %param.10) | copy-start | bytes 196612
  93.3 106.3 %all-reduce.5.cloned.1.call-start = ((), (), s32[]{:S(2)}) async-start(), calls=%async_computation.3 | async-start | bytes 262144 | tf_op jit(solution)/shard_map/psum | solution.py:49
Sparse Core Ops, SparseCore 0:
  93.4 72.9 all-reduce.2
  168.7 30.8 all-reduce.4
